TPU v7x, 32 devices: a whole 2x2x4 slice. The times are simulated.
32 devices in a mesh: parts: 2 (over y), blk: 4 (over x, core), sub: 4 (over z).
Axes of the slice: x: 2, y: 2, z: 4, core: 2. Of those that a mesh axis runs over, the one named last changes fastest.
Arguments:
- tokens: bfloat16 [256, 4096], P(('parts', 'blk'), 'sub'), parts along dimension 0, may hold values from -6 to 6
- expert_ids: int32 [256, 2], P(('parts', 'blk')), parts along dimension 0, may hold values from 0 to 7, all different within a row; in each aligned block of 32 rows (0 to 31, 32 to 63, ...) at most 16 rows name the same one
- gate_level: int32 [256, 2], P(('parts', 'blk')), parts along dimension 0, may hold values from 0 to 15
- gate_weight: bfloat16 [8, 4096, 8192], P('blk', None, 'sub'), may hold values from -0.09375 to 0.09375
- up_weight: bfloat16 [8, 4096, 8192], P('blk', None, 'sub'), may hold values from -0.09375 to 0.09375
- down_weight: bfloat16 [8, 8192, 4096], P('blk', 'sub'), may hold values from -0.0625 to 0.0625
Outputs:
- mixed_out: bfloat16 [256, 4096], P(('parts', 'blk'), 'sub'), parts along dimension 0
There are 2 independent parts, one for each index of `parts`. A program takes and returns all parts, laid end to end along the dimension named above; an argument that names none is the same for every part. Nothing has to cross between parts.
Inputs may be any that keep to these rules, and one draw needn't show every extreme that they name: `expert_ids`: A token's 2 experts differ. Among the 32 tokens of one index of blk (aligned blocks of tokens), no expert is picked by more than 16 tokens, and in some block some expert is picked by exactly 16.
All inputs are finite; a program needn't handle non-finite values.
Results may differ from a plain program's by a relative error of at most 0.015.
Values may be sent and summed in bfloat16 or wider, within the bound.
A program may use at most 192 MiB of HBM per device.

v0:
```python
import functools

import jax
import jax.numpy as jnp
from jax import lax
from jax.sharding import PartitionSpec as P

from jax.experimental import pallas as pl
from jax.experimental.pallas import tpu as pltpu

E = 8
TOP = 2
CAP = 16
BF16 = jnp.bfloat16
F32 = jnp.float32
TILE = 1024
AHEAD = 6


def shards(tokens, expert_ids, gate_level, gate_weight, up_weight, down_weight):
    block_count = lax.axis_size("blk")
    sub_count = lax.axis_size("sub")
    local_slots = gate_weight.shape[0]
    hidden_width = gate_weight.shape[2]
    slot_count = local_slots * block_count
    halves = slot_count // E
    token_rows = tokens.shape[0]
    feature_width = tokens.shape[1]
    buffer_width = slot_count * CAP
    received_rows = block_count * CAP
    picked = expert_ids.reshape(-1)
    onehot = (picked[:, None] == jnp.arange(E, dtype=jnp.int32)[None, :]).astype(jnp.int32)
    ranking = jnp.sum((jnp.cumsum(onehot, axis=0) - onehot) * onehot, axis=1)
    columns = (
        picked[:, None] * CAP
        + (jnp.arange(halves, dtype=jnp.int32) * E)[None, :] * CAP
        + ranking[:, None]
    )
    columns = columns.reshape(token_rows, TOP * halves)
    matches = columns[:, :, None] == jnp.arange(buffer_width, dtype=jnp.int32)[None, None, :]
    levels = gate_level.astype(jnp.float32) + 1.0
    shares = levels / jnp.sum(levels, axis=1, keepdims=True)
    shares_wide = jnp.repeat(shares, halves, axis=1)
    combine_weights = jnp.sum(matches.astype(jnp.float32) * shares_wide[:, :, None], axis=1)
    chosen = jnp.any(matches, axis=1).astype(jnp.bfloat16)
    outgoing = lax.dot_general(
        chosen, tokens, (((0,), (0,)), ((), ())), preferred_element_type=jnp.float32
    )
    outgoing = outgoing.astype(jnp.bfloat16).reshape(slot_count, CAP, feature_width)
    copies = jnp.broadcast_to(
        outgoing.reshape(block_count, 1, local_slots, CAP, feature_width),
        (block_count, sub_count, local_slots, CAP, feature_width),
    )
    copies = copies.reshape(block_count * sub_count, local_slots, CAP, feature_width)
    arrived = lax.all_to_all(copies, ("blk", "sub"), split_axis=0, concat_axis=0, tiled=True)
    arrived = arrived.reshape(block_count, sub_count, local_slots, CAP, feature_width)
    gate_split = gate_weight.reshape(local_slots, sub_count, feature_width, hidden_width)
    up_split = up_weight.reshape(local_slots, sub_count, feature_width, hidden_width)
    gate_acts = jnp.einsum(
        "bsncd,nsdf->nbcf", arrived, gate_split, preferred_element_type=jnp.float32
    )
    up_acts = jnp.einsum("bsncd,nsdf->nbcf", arrived, up_split, preferred_element_type=jnp.float32)
    gate_acts = gate_acts.reshape(local_slots, received_rows, hidden_width)
    up_acts = up_acts.reshape(local_slots, received_rows, hidden_width)
    hidden = (jax.nn.silu(gate_acts) * up_acts).astype(jnp.bfloat16)
    full_out = jnp.einsum("nrf,nfd->nrd", hidden, down_weight, preferred_element_type=jnp.float32)
    local_out = lax.psum_scatter(
        full_out.astype(jnp.bfloat16), "sub", scatter_dimension=2, tiled=True
    )
    home_rows = lax.all_to_all(local_out, "blk", split_axis=1, concat_axis=0, tiled=True)
    home_flat = home_rows.reshape(buffer_width, feature_width).astype(jnp.float32)
    mixed_out = jnp.dot(
        combine_weights,
        home_flat,
        precision=lax.Precision.HIGHEST,
        preferred_element_type=jnp.float32,
    )
    return mixed_out.astype(jnp.bfloat16)


def flip(index, mask, count):
    total, bit = 0, 1
    while bit < count:
        digit = (index // bit) % 2
        total = total + bit * ((1 - digit) if mask & bit else digit)
        bit *= 2
    return total


def fused(
    parts, blks, subs, tokens_hbm, ids, levels, gate_hbm, up_hbm, down_hbm, out,
    taken, picked, rows, gate, up, down, gate_sum, up_sum, hidden, made, home, mixed, landed,
    load_sem, own_sem, tok_send, tok_recv, pick_send, pick_recv, made_send, made_recv, mix_send, mix_recv, relay_send, relay_recv,
):
    plane = parts * blks
    part, blk, sub = lax.axis_index("parts"), lax.axis_index("blk"), lax.axis_index("sub")
    mine = blk * parts + part
    block_rows, width = tokens_hbm.shape
    units = hidden.shape[1]

    def at(slot, depth):
        return {"parts": slot % parts, "blk": slot // parts, "sub": depth}

    near = width // 4
    far = pl.ds(near, width - near)
    quarters = [flip(sub, j, subs) for j in range(subs)]
    peers = [flip(mine, k, plane) for k in range(plane)]

    own = pltpu.make_async_copy(tokens_hbm, taken.at[0], own_sem)
    own.start()
    barrier = pltpu.get_barrier_semaphore()
    for k in range(1, plane):
        pl.semaphore_signal(barrier, inc=1, device_id=at(peers[k], sub), device_id_type=pl.DeviceIdType.MESH)
    for j in range(1, subs):
        pl.semaphore_signal(barrier, inc=1, device_id=at(mine, quarters[j]), device_id_type=pl.DeviceIdType.MESH)

    loads = []
    for j in range(subs):
        span = pl.ds(pl.multiple_of(quarters[j] * width, width), width)
        loads.append(pltpu.make_async_copy(gate_hbm.at[part, span, :], gate.at[j], load_sem.at[2 * j]))
        loads.append(pltpu.make_async_copy(up_hbm.at[part, span, :], up.at[j], load_sem.at[2 * j + 1]))
    for i, j in enumerate(reversed(range(subs))):
        span = pl.ds(pl.multiple_of(quarters[j] * width, width), width)
        loads.append(pltpu.make_async_copy(down_hbm.at[part, :, span], down.at[j], load_sem.at[2 * subs + i]))
    for load in loads[:AHEAD]:
        load.start()

    lines = E * CAP
    line = lax.broadcasted_iota(jnp.int32, (lines, block_rows), 0)
    expert, place = line // CAP, line % CAP
    first = jnp.broadcast_to(ids[0:1, :], (lines, block_rows)) == expert
    second = jnp.broadcast_to(ids[1:2, :], (lines, block_rows)) == expert
    named = jnp.where(first | second, 1.0, 0.0).astype(F32)
    before = lax.broadcasted_iota(jnp.int32, (block_rows, block_rows), 0) < lax.broadcasted_iota(
        jnp.int32, (block_rows, block_rows), 1
    )
    rank = jnp.dot(named.astype(BF16), jnp.where(before, 1.0, 0.0).astype(BF16), preferred_element_type=F32)
    here = jnp.where(rank == place.astype(F32), named, 0.0)
    chosen = here.astype(BF16)

    own.wait()
    pl.semaphore_wait(barrier, plane + subs - 2)

    tok_copies = {}
    for j in range(1, subs):
        tok_copies[j] = pltpu.make_async_remote_copy(
            src_ref=taken.at[0, :, far], dst_ref=taken.at[j, :, far], send_sem=tok_send.at[j], recv_sem=tok_recv.at[j],
            device_id=at(mine, quarters[j]), device_id_type=pl.DeviceIdType.MESH,
        )
        tok_copies[j].start()

    half = width // 2
    spans_in = [(0, 0, near), (0, near, width - near)]
    spans_in += [(j, near, width - near) for j in range(1, subs - 1)]
    spans_in += [(subs - 1, near, half - near), (subs - 1, half, half)]
    spans_out = [(subs - 1, 0, half), (subs - 1, half, half)] + [(j, 0, width) for j in reversed(range(subs - 1))]

    def dispatch(n, j, start, size):
        span = pl.ds(start, size)
        if j > 0 and start == near:
            tok_copies[j].wait_recv()
        sent = jnp.dot(chosen, taken[j, :, span], preferred_element_type=F32)
        picked[j, :, :, span] = sent.astype(BF16).reshape(plane, CAP, size)
        copies = []
        for k in reversed(range(1, plane)):
            copy = pltpu.make_async_remote_copy(
                src_ref=picked.at[j, peers[k], :, span], dst_ref=rows.at[j, mine, :, span],
                send_sem=pick_send.at[n, k], recv_sem=pick_recv.at[n, k],
                device_id=at(peers[k], sub), device_id_type=pl.DeviceIdType.MESH,
            )
            copy.start()
            copies.append(copy)
        rows[j, mine, :, span] = picked[j, mine, :, span]
        return copies

    pick_copies = [dispatch(n, *piece) for n, piece in enumerate(spans_in[:2])]
    for copy in pick_copies[0]:
        copy.wait_recv()
    relays = {}
    for j in range(1, subs):
        relays[j] = pltpu.make_async_remote_copy(
            src_ref=rows.at[0, :, :, pl.ds(0, near)], dst_ref=rows.at[j, :, :, pl.ds(0, near)],
            send_sem=relay_send.at[j], recv_sem=relay_recv.at[j],
            device_id=at(mine, quarters[j]), device_id_type=pl.DeviceIdType.MESH,
        )
        relays[j].start()
    pick_copies += [dispatch(n + 2, *piece) for n, piece in enumerate(spans_in[2:])]

    level = levels[...].astype(F32) + 1.0
    share = level / (level[0:1, :] + level[1:2, :])
    weight = here * jnp.where(
        first,
        jnp.broadcast_to(share[0:1, :], (lines, block_rows)),
        jnp.broadcast_to(share[1:2, :], (lines, block_rows)),
    )
    weight = weight.T
    weight_high = weight.astype(BF16)
    weight_low = (weight - weight_high.astype(F32)).astype(BF16)

    started = AHEAD
    spans_used = [(j, 0, width) for j in range(subs - 1)] + [(subs - 1, 0, half), (subs - 1, half, half)]
    for n, (j, start, size) in enumerate(spans_used):
        if start == 0:
            if j > 0:
                relays[j].wait_recv()
            for i in (2 * j, 2 * j + 1):
                loads[i].wait()
                if started < len(loads):
                    loads[started].start()
                    started += 1
        for copy in pick_copies[n + 1]:
            copy.wait_recv()

        @pl.loop(0, units // TILE)
        def _(step, n=n, j=j, depth=pl.ds(start, size)):
            span = pl.ds(pl.multiple_of(step * TILE, TILE), TILE)
            x = rows[j, :, :, depth].reshape(plane * CAP, depth.size)
            g = jnp.dot(x, gate[j, depth, span], preferred_element_type=F32)
            u = jnp.dot(x, up[j, depth, span], preferred_element_type=F32)
            if n > 0:
                g = g + gate_sum[:, span]
                u = u + up_sum[:, span]
            if n < len(spans_used) - 1:
                gate_sum[:, span] = g
                up_sum[:, span] = u
            else:
                hidden[:, span] = (g / (1.0 + jnp.exp(-g)) * u).astype(BF16)

    made_copies = {}
    mix_copies = {}

    def ship(n, j, span):
        copies = []
        for k in reversed(range(1, plane)):
            copy = pltpu.make_async_remote_copy(
                src_ref=made.at[j, peers[k], :, span], dst_ref=home.at[j, mine, :, span],
                send_sem=made_send.at[n, k], recv_sem=made_recv.at[n, k],
                device_id=at(peers[k], sub), device_id_type=pl.DeviceIdType.MESH,
            )
            copy.start()
            copies.append(copy)
        home[j, mine, :, span] = made[j, mine, :, span]
        made_copies.setdefault(j, []).extend(copies)

    def combine(j):
        for copy in made_copies[j]:
            copy.wait_recv()
        block = home[j].reshape(plane * CAP, width)
        return jnp.dot(weight_high, block, preferred_element_type=F32) + jnp.dot(
            weight_low, block, preferred_element_type=F32
        )

    for n, (j, start, size) in enumerate(spans_out):
        if start == 0:
            loads[2 * subs + subs - 1 - j].wait()
            if started < len(loads):
                loads[started].start()
                started += 1
        step = size // 2

        @pl.loop(0, 2)
        def _(turn, j=j, start=start, step=step):
            span = pl.ds(pl.multiple_of(start + turn * step, step), step)
            y = jnp.dot(hidden[...], down[j, :, span], preferred_element_type=F32)
            made[j, :, :, span] = y.astype(BF16).reshape(plane, CAP, step)

        ship(n, j, pl.ds(start, size))

    for j in reversed(range(1, subs)):
        mixed[j] = combine(j).astype(BF16)
        mix_copies[j] = pltpu.make_async_remote_copy(
            src_ref=mixed.at[j], dst_ref=landed.at[j], send_sem=mix_send.at[j], recv_sem=mix_recv.at[j],
            device_id=at(mine, quarters[j]), device_id_type=pl.DeviceIdType.MESH,
        )
        mix_copies[j].start()
    total = combine(0)
    for j in reversed(range(1, subs)):
        mix_copies[j].wait_recv()
        total = total + landed[j].astype(F32)
    out[...] = total.astype(BF16)

    for j in range(1, subs):
        tok_copies[j].wait_send()
        relays[j].wait_send()
        mix_copies[j].wait_send()
    for copies in pick_copies + list(made_copies.values()):
        for copy in copies:
            copy.wait_send()


def shared_shards(parts, blks, subs, tokens, expert_ids, gate_level, gate_weight, up_weight, down_weight):
    block_rows, width = tokens.shape
    plane = parts * blks
    units = gate_weight.shape[2]
    vmem = pl.BlockSpec(memory_space=pltpu.VMEM)
    hbm = pl.BlockSpec(memory_space=pl.ANY)
    dma = pltpu.SemaphoreType.DMA
    return pl.pallas_call(
        functools.partial(fused, parts, blks, subs),
        out_shape=jax.ShapeDtypeStruct((block_rows, width), BF16),
        in_specs=[hbm, vmem, vmem, hbm, hbm, hbm],
        out_specs=vmem,
        scratch_shapes=[
            pltpu.VMEM((subs, block_rows, width), BF16),
            pltpu.VMEM((subs, plane, CAP, width), BF16),
            pltpu.VMEM((subs, plane, CAP, width), BF16),
            pltpu.VMEM((subs, width, units), BF16),
            pltpu.VMEM((subs, width, units), BF16),
            pltpu.VMEM((subs, units, width), BF16),
            pltpu.VMEM((plane * CAP, units), F32),
            pltpu.VMEM((plane * CAP, units), F32),
            pltpu.VMEM((plane * CAP, units), BF16),
            pltpu.VMEM((subs, plane, CAP, width), BF16),
            pltpu.VMEM((subs, plane, CAP, width), BF16),
            pltpu.VMEM((subs, block_rows, width), BF16),
            pltpu.VMEM((subs, block_rows, width), BF16),
            dma((3 * subs,)), pltpu.SemaphoreType.DMA,
            dma((subs,)), dma((subs,)),
            dma((subs + 2, plane)), dma((subs + 2, plane)),
            dma((subs + 1, plane)), dma((subs + 1, plane)),
            dma((subs,)), dma((subs,)),
            dma((subs,)), dma((subs,)),
        ],
        compiler_params=pltpu.CompilerParams(
            collective_id=0, has_side_effects=True, vmem_limit_bytes=67043328
        ),
    )(tokens, expert_ids.T, gate_level.T, gate_weight, up_weight, down_weight)


def routed(parts, blks, subs, tokens, expert_ids, gate_level, gate_weight, up_weight, down_weight):
    plane = parts * blks
    width = tokens.shape[1]
    units = gate_weight.shape[2]
    fits = gate_weight.shape[0] == parts and plane == E and plane & (plane - 1) == 0
    fits = fits and subs & (subs - 1) == 0 and width % TILE == 0 and units % TILE == 0
    fits = fits and tokens.shape[0] == 2 * CAP
    arrays = (tokens, expert_ids, gate_level, gate_weight, up_weight, down_weight)
    return shared_shards(parts, blks, subs, *arrays) if fits else shards(*arrays)


def solution(mesh):
    sizes = (mesh.shape["parts"], mesh.shape["blk"], mesh.shape["sub"])
    return jax.shard_map(
        functools.partial(routed, *sizes),
        mesh=mesh,
        in_specs=(
            P(("parts", "blk"), "sub"),
            P(("parts", "blk"), None),
            P(("parts", "blk"), None),
            P("blk", None, "sub"),
            P("blk", None, "sub"),
            P("blk", "sub", None),
        ),
        out_specs=P(("parts", "blk"), "sub"),
        check_vma=False,
    )
```

profile of v0, /device:TPU:0, one launch (start us, length us, event | category | flops | bytes accessed | tf_op | source)
XLA Modules:
  0.0 39.6 jit_solution(17642359046459568418)
XLA Ops:
  0.0 38.1 %shard_map.64 = bf16[32,1024]{1,0:T(8,128)(2,1)} custom-call(bf16[32,1024]{1,0:T(8,128)(2,1)} %tokens_hbm.1, s32[2,32]{1,0:T(2,128)} %bitcast.2, s32[2,32]{1,0:T(2,128)} %bitcast.3, bf16[2,4096,2048]{2,1,0:T(8,128)(2,1)} %gate_hbm.1, bf16[2,4096,2048]{2,1,0:T(8,128)(2,1)} %up_hbm.1, bf16[2,2048,4096]{2,1,0:T(8,128)(2,1)} %down_hbm.1), custom_call_target="tpu_custom_call" | custom-call | tf_op jit(solution)/shard_map/pallas_call | solution.py:298
  38.1 1.5 %copy.8 = bf16[32,1024]{1,0:T(8,128)(2,1)} copy(bf16[32,1024]{1,0:T(8,128)(2,1)} %shard_map.64) | data formatting | bytes 131072
where the time goes:
time: 39.7 us; the launch traced here: 39.6 us
  Pallas kernels  38.1 us (96%)
  local copies, waits for them, and re-layouts  1.47 us (4%)
    pallas_call x1, Pallas kernels, shared_shards(): pl.pallas_call(functools.partial(fused, parts, blks, subs), out_shape=jax...  38.1 us
    unnamed x1, local copies, waits for them, and re-layouts  1.47 us

commit v1 on v0

v1 whole, which is shorter than its diff:
```python
import contextlib
import functools

import jax
import jax.numpy as jnp
from jax import lax
from jax.sharding import PartitionSpec as P

from jax.experimental import pallas as pl
from jax.experimental.pallas import tpu as pltpu

E = 8
TOP = 2
CAP = 16
BF16 = jnp.bfloat16
F32 = jnp.float32
TILE = 1024
AHEAD = 3
SCOPES = False


def scope(name):
    return jax.named_scope(name) if SCOPES else contextlib.nullcontext()


def shards(tokens, expert_ids, gate_level, gate_weight, up_weight, down_weight):
    block_count = lax.axis_size("blk")
    sub_count = lax.axis_size("sub")
    local_slots = gate_weight.shape[0]
    hidden_width = gate_weight.shape[2]
    slot_count = local_slots * block_count
    halves = slot_count // E
    token_rows = tokens.shape[0]
    feature_width = tokens.shape[1]
    buffer_width = slot_count * CAP
    received_rows = block_count * CAP
    picked = expert_ids.reshape(-1)
    onehot = (picked[:, None] == jnp.arange(E, dtype=jnp.int32)[None, :]).astype(jnp.int32)
    ranking = jnp.sum((jnp.cumsum(onehot, axis=0) - onehot) * onehot, axis=1)
    columns = (
        picked[:, None] * CAP
        + (jnp.arange(halves, dtype=jnp.int32) * E)[None, :] * CAP
        + ranking[:, None]
    )
    columns = columns.reshape(token_rows, TOP * halves)
    matches = columns[:, :, None] == jnp.arange(buffer_width, dtype=jnp.int32)[None, None, :]
    levels = gate_level.astype(jnp.float32) + 1.0
    shares = levels / jnp.sum(levels, axis=1, keepdims=True)
    shares_wide = jnp.repeat(shares, halves, axis=1)
    combine_weights = jnp.sum(matches.astype(jnp.float32) * shares_wide[:, :, None], axis=1)
    chosen = jnp.any(matches, axis=1).astype(jnp.bfloat16)
    outgoing = lax.dot_general(
        chosen, tokens, (((0,), (0,)), ((), ())), preferred_element_type=jnp.float32
    )
    outgoing = outgoing.astype(jnp.bfloat16).reshape(slot_count, CAP, feature_width)
    copies = jnp.broadcast_to(
        outgoing.reshape(block_count, 1, local_slots, CAP, feature_width),
        (block_count, sub_count, local_slots, CAP, feature_width),
    )
    copies = copies.reshape(block_count * sub_count, local_slots, CAP, feature_width)
    arrived = lax.all_to_all(copies, ("blk", "sub"), split_axis=0, concat_axis=0, tiled=True)
    arrived = arrived.reshape(block_count, sub_count, local_slots, CAP, feature_width)
    gate_split = gate_weight.reshape(local_slots, sub_count, feature_width, hidden_width)
    up_split = up_weight.reshape(local_slots, sub_count, feature_width, hidden_width)
    gate_acts = jnp.einsum(
        "bsncd,nsdf->nbcf", arrived, gate_split, preferred_element_type=jnp.float32
    )
    up_acts = jnp.einsum("bsncd,nsdf->nbcf", arrived, up_split, preferred_element_type=jnp.float32)
    gate_acts = gate_acts.reshape(local_slots, received_rows, hidden_width)
    up_acts = up_acts.reshape(local_slots, received_rows, hidden_width)
    hidden = (jax.nn.silu(gate_acts) * up_acts).astype(jnp.bfloat16)
    full_out = jnp.einsum("nrf,nfd->nrd", hidden, down_weight, preferred_element_type=jnp.float32)
    local_out = lax.psum_scatter(
        full_out.astype(jnp.bfloat16), "sub", scatter_dimension=2, tiled=True
    )
    home_rows = lax.all_to_all(local_out, "blk", split_axis=1, concat_axis=0, tiled=True)
    home_flat = home_rows.reshape(buffer_width, feature_width).astype(jnp.float32)
    mixed_out = jnp.dot(
        combine_weights,
        home_flat,
        precision=lax.Precision.HIGHEST,
        preferred_element_type=jnp.float32,
    )
    return mixed_out.astype(jnp.bfloat16)


def flip(index, mask, count):
    total, bit = 0, 1
    while bit < count:
        digit = (index // bit) % 2
        total = total + bit * ((1 - digit) if mask & bit else digit)
        bit *= 2
    return total


def fused(
    parts, blks, subs, tokens_hbm, ids_hbm, levels_hbm, gate_hbm, up_hbm, down_hbm, out,
    ids, levels, taken, picked, rows, both, down_rest, down_edge, gate_sum, up_sum, hidden, made, home, mixed, landed, edge_sum, edges,
    load_sem, down_sem, own_sem, tok_send, tok_recv, pick_send, pick_recv, made_send, made_recv, mix_send, mix_recv, relay_send, relay_recv, edge_send, edge_recv,
):
    plane = parts * blks
    part, blk, sub = lax.axis_index("parts"), lax.axis_index("blk"), lax.axis_index("sub")
    mine = blk * parts + part
    block_rows, width = tokens_hbm.shape
    units = hidden.shape[1]

    def at(slot, depth):
        return {"parts": slot % parts, "blk": slot // parts, "sub": depth}

    near = width // 4
    far = pl.ds(near, width - near)
    quarters = [flip(sub, j, subs) for j in range(subs)]
    peers = [flip(mine, k, plane) for k in range(plane)]

    def send(source, target, send_sem, recv_sem, to):
        return pltpu.make_async_remote_copy(
            src_ref=source, dst_ref=target, send_sem=send_sem, recv_sem=recv_sem,
            device_id=to, device_id_type=pl.DeviceIdType.MESH,
        )

    def arrived(ref, sem):
        send(ref, ref, sem, sem, at(mine, sub)).wait_recv()

    def departed(ref, sem):
        send(ref, ref, sem, sem, at(mine, sub)).wait_send()

    others = pl.ds(0, plane - 1)
    barrier = pltpu.get_barrier_semaphore()
    for k in range(1, plane):
        pl.semaphore_signal(barrier, inc=1, device_id=at(peers[k], sub), device_id_type=pl.DeviceIdType.MESH)
    for j in range(1, subs):
        pl.semaphore_signal(barrier, inc=1, device_id=at(mine, quarters[j]), device_id_type=pl.DeviceIdType.MESH)
    small = [
        pltpu.make_async_copy(source, target, own_sem.at[n])
        for n, (source, target) in enumerate([(ids_hbm, ids), (levels_hbm, levels), (tokens_hbm, taken.at[0])])
    ]
    for copy in small:
        copy.start()

    slim = width // 4
    edge, rest = pl.ds(0, slim), pl.ds(slim, width - slim)
    loads = []
    for j in range(subs):
        span = pl.ds(pl.multiple_of(quarters[j] * width, width), width)
        loads.append([
            pltpu.make_async_copy(source.at[part, span, :], both.at[i, j], load_sem.at[j])
            for i, source in enumerate((gate_hbm, up_hbm))
        ])
    for j in reversed(range(subs)):
        span = pl.ds(pl.multiple_of(quarters[j] * width + slim, slim), width - slim)
        loads.append([pltpu.make_async_copy(down_hbm.at[part, :, span], down_rest.at[j], down_sem.at[j])])
        if j == subs - 1:
            loads.append([
                pltpu.make_async_copy(
                    down_hbm.at[part, :, pl.ds(pl.multiple_of(quarters[i] * width, width), slim)],
                    down_edge.at[:, pl.ds(i * slim, slim)],
                    down_sem.at[subs],
                )
                for i in range(subs)
            ])

    def load(count):
        for group in loads[:count]:
            for copy in group:
                copy.start()
        del loads[:count]

    for copy in small:
        copy.wait()
    load(AHEAD)

    lines = E * CAP
    line = lax.broadcasted_iota(jnp.int32, (lines, block_rows), 0)
    expert, place = line // CAP, line % CAP
    first = jnp.broadcast_to(ids[0:1, :], (lines, block_rows)) == expert
    second = jnp.broadcast_to(ids[1:2, :], (lines, block_rows)) == expert
    named = jnp.where(first | second, 1.0, 0.0).astype(F32)
    before = lax.broadcasted_iota(jnp.int32, (block_rows, block_rows), 0) < lax.broadcasted_iota(
        jnp.int32, (block_rows, block_rows), 1
    )
    rank = jnp.dot(named.astype(BF16), jnp.where(before, 1.0, 0.0).astype(BF16), preferred_element_type=F32)
    here = jnp.where(rank == place.astype(F32), named, 0.0)
    chosen = here.astype(BF16)

    with scope("barrier"):
        pl.semaphore_wait(barrier, plane + subs - 2)

    tok_copies = {}
    for j in range(1, subs):
        tok_copies[j] = send(
            taken.at[0, :, far], taken.at[j, :, far], tok_send, tok_recv.at[j - 1], at(mine, quarters[j])
        )
        tok_copies[j].start()

    half = width // 2
    spans_in = [(0, 0, near), (0, near, width - near)]
    spans_in += [(j, near, width - near) for j in range(1, subs - 1)]
    spans_in += [(subs - 1, near, half - near), (subs - 1, half, half)]

    def dispatch(n, j, start, size):
        span = pl.ds(start, size)
        if j > 0 and start == near:
            tok_copies[j].wait_recv()
        sent = jnp.dot(chosen, taken[j, :, span], preferred_element_type=F32)
        picked[j, :, :, span] = sent.astype(BF16).reshape(plane, CAP, size)
        for k in reversed(range(1, plane)):
            send(
                picked.at[j, peers[k], :, span], rows.at[j, mine, :, span], pick_send.at[min(n, 1)], pick_recv.at[n], at(peers[k], sub)
            ).start()
        rows[j, mine, :, span] = picked[j, mine, :, span]

    def gathered(n):
        j, start, size = spans_in[n]
        arrived(rows.at[j, others, :, pl.ds(start, size)], pick_recv.at[n])

    for n, piece in enumerate(spans_in[:2]):
        dispatch(n, *piece)
    with scope("pick0"):
        gathered(0)
    relays = {}
    for j in range(1, subs):
        relays[j] = send(
            rows.at[0, :, :, pl.ds(0, near)], rows.at[j, :, :, pl.ds(0, near)],
            relay_send, relay_recv.at[j - 1], at(mine, quarters[j]),
        )
        relays[j].start()
    level = levels[...].astype(F32) + 1.0
    share = level / (level[0:1, :] + level[1:2, :])
    weight = here * jnp.where(
        first,
        jnp.broadcast_to(share[0:1, :], (lines, block_rows)),
        jnp.broadcast_to(share[1:2, :], (lines, block_rows)),
    )
    weight = weight.T
    weight_high = weight.astype(BF16)
    weight_low = (weight - weight_high.astype(F32)).astype(BF16)

    spans_used = [(j, 0, width) for j in range(subs - 1)] + [(subs - 1, 0, half), (subs - 1, half, half)]

    def absorb(n):
        j, start, size = spans_used[n]
        if start == 0:
            if j > 0:
                with scope(f"relay{j}"):
                    relays[j].wait_recv()
            with scope(f"load{j}"):
                arrived(both.at[:, j], load_sem.at[j])
            load(1)
        with scope(f"pick{n + 1}"):
            gathered(n + 1)
        depth = pl.ds(start, size)

        def tile(span):
            x = rows[j, :, :, depth].reshape(plane * CAP, size)
            g = jnp.dot(x, both[0, j, depth, span], preferred_element_type=F32)
            u = jnp.dot(x, both[1, j, depth, span], preferred_element_type=F32)
            if n > 0:
                g = g + gate_sum[:, span]
                u = u + up_sum[:, span]
            if n < len(spans_used) - 1:
                gate_sum[:, span] = g
                up_sum[:, span] = u
            else:
                hidden[:, span] = (g / (1.0 + jnp.exp(-g)) * u).astype(BF16)

        with scope(f"absorb{n}"):
            for step in range(units // TILE):
                tile(pl.ds(step * TILE, TILE))

    for n, piece in enumerate(spans_in[2:]):
        if n == subs - 2:
            absorb(0)
        dispatch(n + 2, *piece)
    for n in range(1, len(spans_used)):
        absorb(n)
    load(len(loads))

    edge_copies = {}
    mix_copies = {}

    def ship(n, j, span):
        for k in reversed(range(1, plane)):
            send(
                made.at[j, peers[k], :, span], home.at[j, mine, :, span], made_send.at[n // subs], made_recv.at[n], at(peers[k], sub)
            ).start()
        home[j, mine, :, span] = made[j, mine, :, span]

    def combine(n, j, span):
        with scope(f"madewait{n}"):
            arrived(home.at[j, others, :, span], made_recv.at[n])
        block = home[j, :, :, span].reshape(plane * CAP, span.size)
        return jnp.dot(weight_high, block, preferred_element_type=F32) + jnp.dot(
            weight_low, block, preferred_element_type=F32
        )

    for j in reversed(range(subs)):
        with scope(f"down{j}"):
            arrived(down_rest.at[j], down_sem.at[j])
            product = jnp.dot(hidden[...], down_rest[j], preferred_element_type=F32)
            made[j, :, :, rest] = product.astype(BF16).reshape(plane, CAP, width - slim)
            ship(j, j, rest)
        if j < subs - 1:
            continue
        with scope("edge"):
            arrived(down_edge, down_sem.at[subs])
            product = jnp.dot(hidden[...], down_edge[...], preferred_element_type=F32)
            edge_sum[...] = product[:, :slim]
            for i in reversed(range(1, subs)):
                made[i, :, :, edge] = product[:, i * slim : (i + 1) * slim].astype(BF16).reshape(plane, CAP, slim)
                edge_copies[i] = send(
                    made.at[i, :, :, edge], edges.at[i], edge_send, edge_recv.at[i - 1], at(mine, quarters[i])
                )
                edge_copies[i].start()

    def mix(j):
        mixed[j] = combine(j, j, rest).astype(BF16)
        mix_copies[j] = send(mixed.at[j], landed.at[j], mix_send, mix_recv.at[j - 1], at(mine, quarters[j]))
        mix_copies[j].start()

    for j in reversed(range(2, subs)):
        mix(j)
    sums = edge_sum[...]
    with scope("edgewait"):
        for j in range(1, subs):
            edge_copies[j].wait_recv()
            sums = sums + edges[j].reshape(plane * CAP, slim).astype(F32)
    made[0, :, :, edge] = sums.astype(BF16).reshape(plane, CAP, slim)
    ship(subs, 0, edge)
    mix(1)
    total = combine(0, 0, rest)
    for j in reversed(range(1, subs)):
        with scope(f"mixwait{j}"):
            mix_copies[j].wait_recv()
        total = total + landed[j].astype(F32)
    out[:, rest] = total.astype(BF16)
    out[:, edge] = combine(subs, 0, edge).astype(BF16)

    with scope("sends"):
        remote = pl.ds(1, subs - 1)
        departed(taken.at[remote, :, far], tok_send)
        departed(rows.at[remote, :, :, pl.ds(0, near)], relay_send)
        departed(edges.at[remote], edge_send)
        departed(landed.at[remote], mix_send)
        departed(rows.at[0, others, :, pl.ds(0, near)], pick_send.at[0])
        departed(rows.at[:, others, :, far], pick_send.at[1])
        departed(home.at[:, others, :, rest], made_send.at[0])
        departed(home.at[0, others, :, edge], made_send.at[1])


def shared_shards(parts, blks, subs, tokens, expert_ids, gate_level, gate_weight, up_weight, down_weight):
    block_rows, width = tokens.shape
    plane = parts * blks
    units = gate_weight.shape[2]
    vmem = pl.BlockSpec(memory_space=pltpu.VMEM)
    hbm = pl.BlockSpec(memory_space=pl.ANY)
    dma = pltpu.SemaphoreType.DMA
    return pl.pallas_call(
        functools.partial(fused, parts, blks, subs),
        out_shape=pltpu.VMEM((block_rows, width), BF16),
        in_specs=[hbm] * 6,
        out_specs=vmem,
        scratch_shapes=[
            pltpu.VMEM(expert_ids.T.shape, jnp.int32),
            pltpu.VMEM(gate_level.T.shape, jnp.int32),
            pltpu.VMEM((subs, block_rows, width), BF16),
            pltpu.VMEM((subs, plane, CAP, width), BF16),
            pltpu.VMEM((subs, plane, CAP, width), BF16),
            pltpu.VMEM((2, subs, width, units), BF16),
            pltpu.VMEM((subs, units, width - width // 4), BF16),
            pltpu.VMEM((units, subs * (width // 4)), BF16),
            pltpu.VMEM((plane * CAP, units), F32),
            pltpu.VMEM((plane * CAP, units), F32),
            pltpu.VMEM((plane * CAP, units), BF16),
            pltpu.VMEM((subs, plane, CAP, width), BF16),
            pltpu.VMEM((subs, plane, CAP, width), BF16),
            pltpu.VMEM((subs, block_rows, width - width // 4), BF16),
            pltpu.VMEM((subs, block_rows, width - width // 4), BF16),
            pltpu.VMEM((plane * CAP, width // 4), F32),
            pltpu.VMEM((subs, plane, CAP, width // 4), BF16),
            dma((subs,)), dma((subs + 1,)), dma((3,)),
            dma, dma((subs - 1,)),
            dma((2,)), dma((subs + 2,)),
            dma((2,)), dma((subs + 1,)),
            dma, dma((subs - 1,)),
            dma, dma((subs - 1,)),
            dma, dma((subs - 1,)),
        ],
        compiler_params=pltpu.CompilerParams(
            collective_id=0, has_side_effects=True, vmem_limit_bytes=65000000
        ),
    )(tokens, expert_ids.T, gate_level.T, gate_weight, up_weight, down_weight)


def routed(parts, blks, subs, tokens, expert_ids, gate_level, gate_weight, up_weight, down_weight):
    plane = parts * blks
    width = tokens.shape[1]
    units = gate_weight.shape[2]
    fits = gate_weight.shape[0] == parts and plane == E and plane & (plane - 1) == 0
    fits = fits and subs & (subs - 1) == 0 and width % TILE == 0 and units % TILE == 0
    fits = fits and tokens.shape[0] == 2 * CAP
    arrays = (tokens, expert_ids, gate_level, gate_weight, up_weight, down_weight)
    return shared_shards(parts, blks, subs, *arrays) if fits else shards(*arrays)


def solution(mesh):
    sizes = (mesh.shape["parts"], mesh.shape["blk"], mesh.shape["sub"])
    return jax.shard_map(
        functools.partial(routed, *sizes),
        mesh=mesh,
        in_specs=(
            P(("parts", "blk"), "sub"),
            P(("parts", "blk"), None),
            P(("parts", "blk"), None),
            P("blk", None, "sub"),
            P("blk", None, "sub"),
            P("blk", "sub", None),
        ),
        out_specs=P(("parts", "blk"), "sub"),
        check_vma=False,
    )
```

time: 39.7 us -> 34 us (0.86)
  Pallas kernels: 38.1 us -> 33.2 us
  local copies, waits for them, and re-layouts: 1.47 us -> 0.63 us
    pallas_call x1, Pallas kernels: 38.1 us -> 33.2 us  [shared_shards(): pl.pallas_call(functools.partial(fused, parts, blks, subs), out_shape=plt...]
    unnamed x1, local copies, waits for them, and re-layouts: 1.47 us -> 0.63 us
where the time goes in v1:
time: 34 us; the launch traced here: 33.9 us
  Pallas kernels  33.2 us (98%)
  local copies, waits for them, and re-layouts  0.63 us (2%)
    pallas_call x1, Pallas kernels, shared_shards(): pl.pallas_call(functools.partial(fused, parts, blks, subs), out_shape=plt...  33.2 us

profile of v1, /device:TPU:0, one launch (start us, length us, event | category | flops | bytes accessed | tf_op | source)
XLA Modules:
  0.0 33.9 jit_solution(5492516786461384879)
XLA Ops:
  0.0 33.2 %shard_map.64 = bf16[32,1024]{1,0:T(8,128)(2,1)S(1)} custom-call(bf16[32,1024]{1,0:T(8,128)(2,1)} %tokens_hbm.1, s32[2,32]{1,0:T(2,128)} %bitcast.2, s32[2,32]{1,0:T(2,128)} %bitcast.3, bf16[2,4096,2048]{2,1,0:T(8,128)(2,1)} %gate_hbm.1, bf16[2,4096,2048]{2,1,0:T(8,128)(2,1)} %up_hbm.1, bf16[2,2048,4096]{2,1,0:T(8,128)(2,1)} %down_hbm.1), custom_call_target="tpu_custom_call" | custom-call | tf_op jit(solution)/shard_map/pallas_call | solution.py:357
  33.2 0.6 %copy.8 = bf16[32,1024]{1,0:T(8,128)(2,1)} copy(bf16[32,1024]{1,0:T(8,128)(2,1)S(1)} %shard_map.64) | data formatting | bytes 131072

commit v2 on v1

--- a/solution.py
+++ b/solution.py
@@ -16,6 +16,8 @@
 F32 = jnp.float32
 TILE = 1024
 AHEAD = 3
+NEAR = 2
+SLIM = 2
 SCOPES = False
 
 
@@ -95,7 +97,7 @@
 
 def fused(
     parts, blks, subs, tokens_hbm, ids_hbm, levels_hbm, gate_hbm, up_hbm, down_hbm, out,
-    ids, levels, taken, picked, rows, both, down_rest, down_edge, gate_sum, up_sum, hidden, made, home, mixed, landed, edge_sum, edges,
+    ids, levels, taken, picked, rows, both, down_rest, down_edge, gate_sum, up_sum, hidden, made, home, mixed, landed, edge_sum, edges, placed,
     load_sem, down_sem, own_sem, tok_send, tok_recv, pick_send, pick_recv, made_send, made_recv, mix_send, mix_recv, relay_send, relay_recv, edge_send, edge_recv,
 ):
     plane = parts * blks
@@ -107,7 +109,7 @@
     def at(slot, depth):
         return {"parts": slot % parts, "blk": slot // parts, "sub": depth}
 
-    near = width // 4
+    near = width * NEAR // 8
     far = pl.ds(near, width - near)
     quarters = [flip(sub, j, subs) for j in range(subs)]
     peers = [flip(mine, k, plane) for k in range(plane)]
@@ -137,7 +139,7 @@
     for copy in small:
         copy.start()
 
-    slim = width // 4
+    slim = width * SLIM // 8
     edge, rest = pl.ds(0, slim), pl.ds(slim, width - slim)
     loads = []
     for j in range(subs):
@@ -146,18 +148,17 @@
             pltpu.make_async_copy(source.at[part, span, :], both.at[i, j], load_sem.at[j])
             for i, source in enumerate((gate_hbm, up_hbm))
         ])
+    loads.append([
+        pltpu.make_async_copy(
+            down_hbm.at[part, :, pl.ds(pl.multiple_of(quarters[j] * width, width), slim)],
+            down_edge.at[:, pl.ds((subs - 1 - j) * slim, slim)],
+            down_sem.at[subs],
+        )
+        for j in range(subs)
+    ])
     for j in reversed(range(subs)):
         span = pl.ds(pl.multiple_of(quarters[j] * width + slim, slim), width - slim)
         loads.append([pltpu.make_async_copy(down_hbm.at[part, :, span], down_rest.at[j], down_sem.at[j])])
-        if j == subs - 1:
-            loads.append([
-                pltpu.make_async_copy(
-                    down_hbm.at[part, :, pl.ds(pl.multiple_of(quarters[i] * width, width), slim)],
-                    down_edge.at[:, pl.ds(i * slim, slim)],
-                    down_sem.at[subs],
-                )
-                for i in range(subs)
-            ])
 
     def load(count):
         for group in loads[:count]:
@@ -181,7 +182,29 @@
     rank = jnp.dot(named.astype(BF16), jnp.where(before, 1.0, 0.0).astype(BF16), preferred_element_type=F32)
     here = jnp.where(rank == place.astype(F32), named, 0.0)
     chosen = here.astype(BF16)
-
+    placed[...] = here
+
+    half = width // 2
+    spans_in = [(0, 0, near), (0, near, width - near)]
+    for j in range(1, subs):
+        spans_in += [(j, half, half), (j, near, half - near)]
+
+    def pick(j, start, size):
+        span = pl.ds(start, size)
+        sent = jnp.dot(chosen, taken[j, :, span], preferred_element_type=F32)
+        picked[j, :, :, span] = sent.astype(BF16).reshape(plane, CAP, size)
+
+    def spread(n):
+        j, start, size = spans_in[n]
+        span = pl.ds(start, size)
+        for k in reversed(range(1, plane)):
+            send(
+                picked.at[j, peers[k], :, span], rows.at[j, mine, :, span],
+                pick_send.at[min(n, 1)], pick_recv.at[n], at(peers[k], sub),
+            ).start()
+        rows[j, mine, :, span] = picked[j, mine, :, span]
+
+    pick(0, 0, width)
     with scope("barrier"):
         pl.semaphore_wait(barrier, plane + subs - 2)
 
@@ -191,30 +214,13 @@
             taken.at[0, :, far], taken.at[j, :, far], tok_send, tok_recv.at[j - 1], at(mine, quarters[j])
         )
         tok_copies[j].start()
-
-    half = width // 2
-    spans_in = [(0, 0, near), (0, near, width - near)]
-    spans_in += [(j, near, width - near) for j in range(1, subs - 1)]
-    spans_in += [(subs - 1, near, half - near), (subs - 1, half, half)]
-
-    def dispatch(n, j, start, size):
-        span = pl.ds(start, size)
-        if j > 0 and start == near:
-            tok_copies[j].wait_recv()
-        sent = jnp.dot(chosen, taken[j, :, span], preferred_element_type=F32)
-        picked[j, :, :, span] = sent.astype(BF16).reshape(plane, CAP, size)
-        for k in reversed(range(1, plane)):
-            send(
-                picked.at[j, peers[k], :, span], rows.at[j, mine, :, span], pick_send.at[min(n, 1)], pick_recv.at[n], at(peers[k], sub)
-            ).start()
-        rows[j, mine, :, span] = picked[j, mine, :, span]
+    spread(0)
+    spread(1)
 
     def gathered(n):
         j, start, size = spans_in[n]
         arrived(rows.at[j, others, :, pl.ds(start, size)], pick_recv.at[n])
 
-    for n, piece in enumerate(spans_in[:2]):
-        dispatch(n, *piece)
     with scope("pick0"):
         gathered(0)
     relays = {}
@@ -224,30 +230,24 @@
             relay_send, relay_recv.at[j - 1], at(mine, quarters[j]),
         )
         relays[j].start()
-    level = levels[...].astype(F32) + 1.0
-    share = level / (level[0:1, :] + level[1:2, :])
-    weight = here * jnp.where(
-        first,
-        jnp.broadcast_to(share[0:1, :], (lines, block_rows)),
-        jnp.broadcast_to(share[1:2, :], (lines, block_rows)),
-    )
-    weight = weight.T
-    weight_high = weight.astype(BF16)
-    weight_low = (weight - weight_high.astype(F32)).astype(BF16)
-
-    spans_used = [(j, 0, width) for j in range(subs - 1)] + [(subs - 1, 0, half), (subs - 1, half, half)]
+    spans_used = [(0, 0, width, 1)]
+    for j in range(1, subs - 1):
+        spans_used += [(j, half, half, 2 * j), (j, 0, half, 2 * j + 1)]
+    last = 2 * (subs - 1)
+    spans_used += [(subs - 1, half, half, last), (subs - 1, 0, near, None), (subs - 1, near, half - near, last + 1)]
 
     def absorb(n):
-        j, start, size = spans_used[n]
-        if start == 0:
-            if j > 0:
-                with scope(f"relay{j}"):
-                    relays[j].wait_recv()
+        j, start, size, source = spans_used[n]
+        if start == half or j == 0:
             with scope(f"load{j}"):
                 arrived(both.at[:, j], load_sem.at[j])
-            load(1)
-        with scope(f"pick{n + 1}"):
-            gathered(n + 1)
+            load(2)
+        if start == 0 and j > 0:
+            with scope(f"relay{j}"):
+                relays[j].wait_recv()
+        if source is not None:
+            with scope(f"pick{source}"):
+                gathered(source)
         depth = pl.ds(start, size)
 
         def tile(span):
@@ -267,13 +267,21 @@
             for step in range(units // TILE):
                 tile(pl.ds(step * TILE, TILE))
 
-    for n, piece in enumerate(spans_in[2:]):
-        if n == subs - 2:
+    for j in range(1, subs):
+        if j == subs - 1:
             absorb(0)
-        dispatch(n + 2, *piece)
-    for n in range(1, len(spans_used)):
+        with scope(f"tok{j}"):
+            tok_copies[j].wait_recv()
+        pick(j, near, width - near)
+        spread(2 * j)
+        spread(2 * j + 1)
+    for n in range(1, len(spans_used) - 1):
         absorb(n)
     load(len(loads))
+    with scope("downwait"):
+        arrived(down_edge, down_sem.at[subs])
+        arrived(down_rest.at[subs - 1], down_sem.at[subs - 1])
+    absorb(len(spans_used) - 1)
 
     edge_copies = {}
     mix_copies = {}
@@ -281,39 +289,75 @@
     def ship(n, j, span):
         for k in reversed(range(1, plane)):
             send(
-                made.at[j, peers[k], :, span], home.at[j, mine, :, span], made_send.at[n // subs], made_recv.at[n], at(peers[k], sub)
+                made.at[j, peers[k], :, span], home.at[j, mine, :, span],
+                made_send.at[1 if n == subs else 0], made_recv.at[n], at(peers[k], sub),
             ).start()
         home[j, mine, :, span] = made[j, mine, :, span]
 
-    def combine(n, j, span):
-        with scope(f"madewait{n}"):
+    def collect(n, j, span):
+        with scope(f"made{n}"):
             arrived(home.at[j, others, :, span], made_recv.at[n])
+
+    def combine(j, span):
         block = home[j, :, :, span].reshape(plane * CAP, span.size)
         return jnp.dot(weight_high, block, preferred_element_type=F32) + jnp.dot(
             weight_low, block, preferred_element_type=F32
         )
 
-    for j in reversed(range(subs)):
+    def strip(first, count):
+        begin = subs - 1 - first
+        product = jnp.dot(
+            hidden[...], down_edge[:, begin * slim : (begin + count) * slim], preferred_element_type=F32
+        )
+        for n, i in enumerate(range(first, first - count, -1)):
+            part_sum = product[:, n * slim : (n + 1) * slim]
+            if i == 0:
+                edge_sum[...] = part_sum
+                continue
+            made[i, :, :, edge] = part_sum.astype(BF16).reshape(plane, CAP, slim)
+            edge_copies[i] = send(
+                made.at[i, :, :, edge], edges.at[i], edge_send, edge_recv.at[i - 1], at(mine, quarters[i])
+            )
+            edge_copies[i].start()
+
+    def project(n, j, start, size):
+        product = jnp.dot(hidden[...], down_rest[j, :, start - slim : start - slim + size], preferred_element_type=F32)
+        made[j, :, :, pl.ds(start, size)] = product.astype(BF16).reshape(plane, CAP, size)
+        ship(n, j, pl.ds(start, size))
+
+    top = subs - 1
+    with scope("strip0"):
+        strip(top, subs // 2)
+    with scope("proj0"):
+        project(subs + 1, top, slim, half)
+    with scope("strip1"):
+        strip(top - subs // 2, subs - subs // 2)
+    with scope("proj1"):
+        project(top, top, slim + half, width - slim - half)
+    for j in reversed(range(top)):
         with scope(f"down{j}"):
             arrived(down_rest.at[j], down_sem.at[j])
-            product = jnp.dot(hidden[...], down_rest[j], preferred_element_type=F32)
-            made[j, :, :, rest] = product.astype(BF16).reshape(plane, CAP, width - slim)
-            ship(j, j, rest)
-        if j < subs - 1:
-            continue
-        with scope("edge"):
-            arrived(down_edge, down_sem.at[subs])
-            product = jnp.dot(hidden[...], down_edge[...], preferred_element_type=F32)
-            edge_sum[...] = product[:, :slim]
-            for i in reversed(range(1, subs)):
-                made[i, :, :, edge] = product[:, i * slim : (i + 1) * slim].astype(BF16).reshape(plane, CAP, slim)
-                edge_copies[i] = send(
-                    made.at[i, :, :, edge], edges.at[i], edge_send, edge_recv.at[i - 1], at(mine, quarters[i])
-                )
-                edge_copies[i].start()
+            project(j, j, slim, width - slim)
+
+    first = jnp.broadcast_to(ids[0:1, :], (lines, block_rows)) == line // CAP
+    level = levels[...].astype(F32) + 1.0
+    share = level / (level[0:1, :] + level[1:2, :])
+    weight = placed[...] * jnp.where(
+        first,
+        jnp.broadcast_to(share[0:1, :], (lines, block_rows)),
+        jnp.broadcast_to(share[1:2, :], (lines, block_rows)),
+    )
+    weight = weight.T
+    weight_high = weight.astype(BF16)
+    weight_low = (weight - weight_high.astype(F32)).astype(BF16)
 
     def mix(j):
-        mixed[j] = combine(j, j, rest).astype(BF16)
+        if j == top:
+            collect(subs + 1, j, pl.ds(slim, half))
+            collect(j, j, pl.ds(slim + half, width - slim - half))
+        else:
+            collect(j, j, rest)
+        mixed[j] = combine(j, rest).astype(BF16)
         mix_copies[j] = send(mixed.at[j], landed.at[j], mix_send, mix_recv.at[j - 1], at(mine, quarters[j]))
         mix_copies[j].start()
 
@@ -327,13 +371,15 @@
     made[0, :, :, edge] = sums.astype(BF16).reshape(plane, CAP, slim)
     ship(subs, 0, edge)
     mix(1)
-    total = combine(0, 0, rest)
+    collect(0, 0, rest)
+    total = combine(0, rest)
     for j in reversed(range(1, subs)):
         with scope(f"mixwait{j}"):
             mix_copies[j].wait_recv()
         total = total + landed[j].astype(F32)
     out[:, rest] = total.astype(BF16)
-    out[:, edge] = combine(subs, 0, edge).astype(BF16)
+    collect(subs, 0, edge)
+    out[:, edge] = combine(0, edge).astype(BF16)
 
     with scope("sends"):
         remote = pl.ds(1, subs - 1)
@@ -366,21 +412,22 @@
             pltpu.VMEM((subs, plane, CAP, width), BF16),
             pltpu.VMEM((subs, plane, CAP, width), BF16),
             pltpu.VMEM((2, subs, width, units), BF16),
-            pltpu.VMEM((subs, units, width - width // 4), BF16),
-            pltpu.VMEM((units, subs * (width // 4)), BF16),
+            pltpu.VMEM((subs, units, width - width * SLIM // 8), BF16),
+            pltpu.VMEM((units, subs * (width * SLIM // 8)), BF16),
             pltpu.VMEM((plane * CAP, units), F32),
             pltpu.VMEM((plane * CAP, units), F32),
             pltpu.VMEM((plane * CAP, units), BF16),
             pltpu.VMEM((subs, plane, CAP, width), BF16),
             pltpu.VMEM((subs, plane, CAP, width), BF16),
-            pltpu.VMEM((subs, block_rows, width - width // 4), BF16),
-            pltpu.VMEM((subs, block_rows, width - width // 4), BF16),
-            pltpu.VMEM((plane * CAP, width // 4), F32),
-            pltpu.VMEM((subs, plane, CAP, width // 4), BF16),
+            pltpu.VMEM((subs, block_rows, width - width * SLIM // 8), BF16),
+            pltpu.VMEM((subs, block_rows, width - width * SLIM // 8), BF16),
+            pltpu.VMEM((plane * CAP, width * SLIM // 8), F32),
+            pltpu.VMEM((subs, plane, CAP, width * SLIM // 8), BF16),
+            pltpu.VMEM((E * CAP, block_rows), F32),
             dma((subs,)), dma((subs + 1,)), dma((3,)),
             dma, dma((subs - 1,)),
+            dma((2,)), dma((2 * subs,)),
             dma((2,)), dma((subs + 2,)),
-            dma((2,)), dma((subs + 1,)),
             dma, dma((subs - 1,)),
             dma, dma((subs - 1,)),
             dma, dma((subs - 1,)),
@@ -396,7 +443,7 @@
     width = tokens.shape[1]
     units = gate_weight.shape[2]
     fits = gate_weight.shape[0] == parts and plane == E and plane & (plane - 1) == 0
-    fits = fits and subs & (subs - 1) == 0 and width % TILE == 0 and units % TILE == 0
+    fits = fits and subs > 1 and subs & (subs - 1) == 0 and width % TILE == 0 and units % TILE == 0
     fits = fits and tokens.shape[0] == 2 * CAP
     arrays = (tokens, expert_ids, gate_level, gate_weight, up_weight, down_weight)
     return shared_shards(parts, blks, subs, *arrays) if fits else shards(*arrays)

time: 34 us -> 32.5 us (0.956)
  Pallas kernels: 33.2 us -> 31.7 us
    pallas_call x1, Pallas kernels: 33.2 us -> 31.7 us  [shared_shards(): pl.pallas_call(functools.partial(fused, parts, blks, subs), out_shape=plt...]
where the time goes in v2:
time: 32.5 us; the launch traced here: 32.4 us
  Pallas kernels  31.7 us (98%)
  local copies, waits for them, and re-layouts  0.63 us (2%)
    pallas_call x1, Pallas kernels, shared_shards(): pl.pallas_call(functools.partial(fused, parts, blks, subs), out_shape=plt...  31.7 us

profile of v2, /device:TPU:0, one launch (start us, length us, event | category | flops | bytes accessed | tf_op | source)
XLA Modules:
  0.0 32.4 jit_solution(7336054857729464141)
XLA Ops:
  0.0 31.7 %shard_map.64 = bf16[32,1024]{1,0:T(8,128)(2,1)S(1)} custom-call(bf16[32,1024]{1,0:T(8,128)(2,1)} %tokens_hbm.1, s32[2,32]{1,0:T(2,128)} %bitcast.2, s32[2,32]{1,0:T(2,128)} %bitcast.3, bf16[2,4096,2048]{2,1,0:T(8,128)(2,1)} %gate_hbm.1, bf16[2,4096,2048]{2,1,0:T(8,128)(2,1)} %up_hbm.1, bf16[2,2048,4096]{2,1,0:T(8,128)(2,1)} %down_hbm.1), custom_call_target="tpu_custom_call" | custom-call | tf_op jit(solution)/shard_map/pallas_call | solution.py:403
  31.8 0.6 %copy.8 = bf16[32,1024]{1,0:T(8,128)(2,1)} copy(bf16[32,1024]{1,0:T(8,128)(2,1)S(1)} %shard_map.64) | data formatting | bytes 131072

commit v3 on v2

--- a/solution.py
+++ b/solution.py
@@ -168,7 +168,6 @@
 
     for copy in small:
         copy.wait()
-    load(AHEAD)
 
     lines = E * CAP
     line = lax.broadcasted_iota(jnp.int32, (lines, block_rows), 0)
@@ -204,7 +203,8 @@
             ).start()
         rows[j, mine, :, span] = picked[j, mine, :, span]
 
-    pick(0, 0, width)
+    pick(0, 0, near)
+    load(AHEAD)
     with scope("barrier"):
         pl.semaphore_wait(barrier, plane + subs - 2)
 
@@ -215,6 +215,7 @@
         )
         tok_copies[j].start()
     spread(0)
+    pick(0, near, width - near)
     spread(1)
 
     def gathered(n):
@@ -337,7 +338,11 @@
     for j in reversed(range(top)):
         with scope(f"down{j}"):
             arrived(down_rest.at[j], down_sem.at[j])
-            project(j, j, slim, width - slim)
+            if j == 1:
+                project(subs + 2, j, slim, half)
+                project(j, j, slim + half, width - slim - half)
+            else:
+                project(j, j, slim, width - slim)
 
     first = jnp.broadcast_to(ids[0:1, :], (lines, block_rows)) == line // CAP
     level = levels[...].astype(F32) + 1.0
@@ -351,15 +356,26 @@
     weight_high = weight.astype(BF16)
     weight_low = (weight - weight_high.astype(F32)).astype(BF16)
 
+    def post(j, m, start, size):
+        span = pl.ds(start - slim, size)
+        mixed[j, :, span] = combine(j, pl.ds(start, size)).astype(BF16)
+        copy = send(mixed.at[j, :, span], landed.at[j, :, span], mix_send, mix_recv.at[m], at(mine, quarters[j]))
+        copy.start()
+        mix_copies.setdefault(j, []).append(copy)
+
     def mix(j):
+        if j == 1:
+            collect(subs + 2, j, pl.ds(slim, half))
+            post(j, 0, slim, half)
+            collect(j, j, pl.ds(slim + half, width - slim - half))
+            post(j, subs - 1, slim + half, width - slim - half)
+            return
         if j == top:
             collect(subs + 1, j, pl.ds(slim, half))
             collect(j, j, pl.ds(slim + half, width - slim - half))
         else:
             collect(j, j, rest)
-        mixed[j] = combine(j, rest).astype(BF16)
-        mix_copies[j] = send(mixed.at[j], landed.at[j], mix_send, mix_recv.at[j - 1], at(mine, quarters[j]))
-        mix_copies[j].start()
+        post(j, j - 1, slim, width - slim)
 
     for j in reversed(range(2, subs)):
         mix(j)
@@ -375,7 +391,8 @@
     total = combine(0, rest)
     for j in reversed(range(1, subs)):
         with scope(f"mixwait{j}"):
-            mix_copies[j].wait_recv()
+            for copy in mix_copies[j]:
+                copy.wait_recv()
         total = total + landed[j].astype(F32)
     out[:, rest] = total.astype(BF16)
     collect(subs, 0, edge)
@@ -427,8 +444,8 @@
             dma((subs,)), dma((subs + 1,)), dma((3,)),
             dma, dma((subs - 1,)),
             dma((2,)), dma((2 * subs,)),
-            dma((2,)), dma((subs + 2,)),
-            dma, dma((subs - 1,)),
+            dma((2,)), dma((subs + 3,)),
+            dma, dma((subs,)),
             dma, dma((subs - 1,)),
             dma, dma((subs - 1,)),
         ],
@@ -443,7 +460,7 @@
     width = tokens.shape[1]
     units = gate_weight.shape[2]
     fits = gate_weight.shape[0] == parts and plane == E and plane & (plane - 1) == 0
-    fits = fits and subs > 1 and subs & (subs - 1) == 0 and width % TILE == 0 and units % TILE == 0
+    fits = fits and subs > 2 and subs & (subs - 1) == 0 and width % TILE == 0 and units % TILE == 0
     fits = fits and tokens.shape[0] == 2 * CAP
     arrays = (tokens, expert_ids, gate_level, gate_weight, up_weight, down_weight)
     return shared_shards(parts, blks, subs, *arrays) if fits else shards(*arrays)

time: 32.5 us -> 32.4 us (level)
  no operation moved by 1% of the time
where the time goes in v3:
time: 32.4 us; the launch traced here: 32.2 us
  Pallas kernels  31.6 us (98%)
  local copies, waits for them, and re-layouts  0.63 us (2%)
    pallas_call x1, Pallas kernels, shared_shards(): pl.pallas_call(functools.partial(fused, parts, blks, subs), out_shape=plt...  31.6 us

profile of v3, /device:TPU:0, one launch (start us, length us, event | category | flops | bytes accessed | tf_op | source)
XLA Modules:
  0.0 32.2 jit_solution(10549205998163013129)
XLA Ops:
  0.0 31.6 %shard_map.64 = bf16[32,1024]{1,0:T(8,128)(2,1)S(1)} custom-call(bf16[32,1024]{1,0:T(8,128)(2,1)} %tokens_hbm.1, s32[2,32]{1,0:T(2,128)} %bitcast.2, s32[2,32]{1,0:T(2,128)} %bitcast.3, bf16[2,4096,2048]{2,1,0:T(8,128)(2,1)} %gate_hbm.1, bf16[2,4096,2048]{2,1,0:T(8,128)(2,1)} %up_hbm.1, bf16[2,2048,4096]{2,1,0:T(8,128)(2,1)} %down_hbm.1), custom_call_target="tpu_custom_call" | custom-call | tf_op jit(solution)/shard_map/pallas_call | solution.py:420
  31.6 0.6 %copy.8 = bf16[32,1024]{1,0:T(8,128)(2,1)} copy(bf16[32,1024]{1,0:T(8,128)(2,1)S(1)} %shard_map.64) | data formatting | bytes 131072
